TPU v7x, 256 devices: a whole 4x4x8 slice. The times are simulated.
256 devices in a mesh: expert: 16 (over x, y), tensor: 8 (over z), replica: 2 (over core).
Axes of the slice: x: 4, y: 4, z: 8, core: 2. Of those that a mesh axis runs over, the one named last changes fastest.
Arguments:
- trained: float32 [16, 7168, 2048], P('replica', 'tensor', 'expert'), may hold values from -3080 to 3080
- snapshot: bfloat16 [16, 7168, 2048], P('replica', 'tensor', 'expert'), may hold values from -3072 to 3072
- changed: int32 [16, 56, 16], P('replica', 'tensor', 'expert'), may hold values from 0 to 1, as said below
- placement: int32 [16], replicated, may hold values from 0 to 15, each once
Outputs:
- rotated_update: bfloat16 [16, 7168, 2048], P('expert', None, 'tensor')
Inputs may be any that keep to these rules, and one draw needn't show every extreme that they name: `placement`: each of the 16 experts appears exactly once. `changed`: in each aligned block of 7 block rows by 1 block columns of one expert, at most 4 entries are 1; for every expert some such block has exactly 4.
All inputs are finite; a program needn't handle non-finite values.
Results may differ from a plain program's by a relative error of at most 0.001.
Values may be sent and summed in bfloat16 or wider, within the bound.
A program may use at most 64 MiB of HBM per device.

v0:
```python
import math
import jax
import jax.numpy as jnp
from jax import lax
from jax.sharding import PartitionSpec as P

BLK = 128


def hadamard():
    positions = jnp.arange(BLK, dtype=jnp.int32)
    parity = jnp.zeros((BLK, BLK), jnp.int32)
    for bit_level in range(BLK.bit_length() - 1):
        parity = parity + (positions[:, None] >> bit_level & 1) * (
            positions[None, :] >> bit_level & 1
        )
    return (1 - 2 * (parity % 2)).astype(jnp.float32) / math.sqrt(BLK)


def body(trained, snapshot, changed, placement):
    hadamard_table = hadamard()
    local_experts, local_rows, local_cols = trained.shape
    copies = lax.axis_size("replica")
    tensor_count = lax.axis_size("tensor")
    expert_count = lax.axis_size("expert")
    members = expert_count // tensor_count
    slot_total = placement.shape[0]
    owner_slots = slot_total // expert_count
    block_rows = local_rows // BLK
    block_cols = local_cols // BLK
    part_rows = BLK // copies
    block_count = block_rows * block_cols
    capacity = (4 * block_count + 3) // 7
    block_flags = changed.reshape(local_experts, block_count)
    position = jnp.arange(block_count, dtype=jnp.int32)
    ranking = jnp.where(block_flags == 1, position[None, :], block_count + position[None, :])
    picked = jnp.argsort(ranking, axis=1)[:, :capacity]
    used_slots = jnp.take_along_axis(block_flags, picked, axis=1)
    expert_ids = jnp.arange(local_experts, dtype=jnp.int32)[:, None]
    row_ids = picked // block_cols
    col_ids = picked % block_cols
    new_tiles = trained.reshape(local_experts, block_rows, BLK, block_cols, BLK)[
        expert_ids, row_ids, :, col_ids, :
    ]
    old_tiles = snapshot.reshape(local_experts, block_rows, BLK, block_cols, BLK)[
        expert_ids, row_ids, :, col_ids, :
    ]
    delta_tiles = jnp.where(
        used_slots[:, :, None, None] == 1, new_tiles - old_tiles.astype(jnp.float32), 0.0
    )
    coded_tiles = jnp.einsum(
        "ij,pmjk->pmik", hadamard_table, delta_tiles, precision=lax.Precision.HIGHEST
    ).astype(jnp.bfloat16)
    coded_tiles = coded_tiles.reshape(local_experts, capacity, copies, part_rows, BLK)
    spots_pair = jnp.broadcast_to(picked[:, :, None], (local_experts, capacity, copies))
    tiles_all, spots_all = (
        lax.all_to_all(coded_tiles, "replica", split_axis=2, concat_axis=0, tiled=True),
        lax.all_to_all(spots_pair, "replica", split_axis=2, concat_axis=0, tiled=True),
    )
    chosen = jnp.take(tiles_all, placement, axis=0).reshape(
        slot_total, 1, 1, capacity, part_rows, BLK
    )
    chosen_spots = jnp.take(spots_all, placement, axis=0).reshape(slot_total, 1, 1, capacity)
    tiles_in, spot_numbers = (
        lax.all_to_all(
            lax.all_to_all(chosen, "expert", split_axis=0, concat_axis=2, tiled=True),
            "tensor",
            split_axis=2,
            concat_axis=1,
            tiled=True,
        ),
        lax.all_to_all(
            lax.all_to_all(chosen_spots, "expert", split_axis=0, concat_axis=2, tiled=True),
            "tensor",
            split_axis=2,
            concat_axis=1,
            tiled=True,
        ),
    )
    source_count = tiles_in.shape[1]
    one_hot = (spot_numbers[..., None] == position).astype(jnp.bfloat16)
    placed = jnp.einsum(
        "osnmg,osnmab->osngab", one_hot, tiles_in, preferred_element_type=jnp.float32
    ).astype(jnp.bfloat16)
    placed = placed.reshape(
        owner_slots, source_count, members, block_rows, block_cols, part_rows, BLK
    )
    placed = jnp.transpose(placed, (0, 1, 3, 5, 2, 4, 6))
    owner_cols = members * block_cols * BLK
    owned_rows = placed.reshape(owner_slots, source_count, block_rows, 1, part_rows, owner_cols)
    whole_rows = lax.all_gather(owned_rows, "replica", axis=3, tiled=True)
    return whole_rows.reshape(owner_slots, tensor_count * block_rows * BLK, owner_cols)


def solution(mesh):
    in_specs = (
        P("replica", "tensor", "expert"),
        P("replica", "tensor", "expert"),
        P("replica", "tensor", "expert"),
        P(),
    )
    out_specs = P("expert", None, "tensor")
    return jax.shard_map(body, mesh=mesh, in_specs=in_specs, out_specs=out_specs, check_vma=False)
```

profile of v0, /device:TPU:1, one launch (start us, length us, event | category | flops | bytes accessed | tf_op | source)
XLA Modules:
  0.0 145.1 jit_solution(11660733728816668597)
XLA Ops:
  6.5 0.0 copy-start
  6.5 0.9 iota_select_fusion
  7.4 0.7 sort.17
  8.1 0.6 broadcast_in_dim.55
  8.7 6.4 %all-to-all-start = ((s32[8,4,2]{0,1,2:T(4,128)}), s32[8,4,2]{0,1,2:T(4,128)S(1)}, u32[]{:S(2)}, u32[]{:S(2)}) async-start(s32[8,4,2]{0,1,2:T(4,128)} %broadcast_in_dim.55), calls=%async_computation | async-start | bytes 8192 | tf_op jit(solution)/shard_map/all_to_all | solution.py:58
  15.1 0.7 compare_and_fusion
  15.8 0.7 compare_select_fusion.1
  16.4 0.8 copy.38
  17.2 0.1 copy.46
  17.3 0.1 reshape.261
  17.4 0.7 gather_fusion.4
  18.1 0.1 reshape.264
  18.1 0.1 copy.47
  18.2 0.1 copy.48
  18.3 0.0 copy-done
  18.3 0.8 gather_fusion.2
  19.1 4.0 %gather_fusion.1 = f32[32,128,128]{2,1,0:T(8,128)} fusion(f32[8,7,128,1,128]{4,2,1,0,3:T(8,128)} %bitcast.67, s32[32]{0:T(128)S(1)} %reshape.261), kind=kCustom, calls=%fused_computation.1 | custom fusion | bytes 4194688 | tf_op jit(solution)/shard_map/gather | solution.py:42
  23.2 1.9 %convert_subtract_fusion = f32[32,128,128]{2,1,0:T(8,128)S(1)} fusion(f32[32,128,128]{2,1,0:T(8,128)} %gather_fusion.1, bf16[32,128,128]{2,1,0:T(8,128)(2,1)S(1)} %gather_fusion.2), kind=kLoop, calls=%fused_computation.5 | loop fusion | flops 1048576 | bytes 5242880 | tf_op jit(solution)/shard_map/sub | solution.py:49
  25.0 2.3 %fusion.2 = bf16[8,4,128,128]{2,3,1,0:T(8,128)(2,1)S(1)} fusion(f32[8,4,128,128]{3,2,1,0:T(8,128)S(1)} %bitcast.61, pred[8,4]{1,0:T(8,128)(4,1)S(1)} %copy.48, s32[128]{0:T(128)S(1)} %get-tuple-element.7, s32[128]{0:T(128)S(1)} %get-tuple-element.8, s32[128]{0:T(128)S(1)} %get-tuple-element.9, s32[128]{0:T(128)S(1)} %get-tuple-element.10, ...), kind=kOutput, calls=%fused_computation.9 | convolution fusion | flops 806813696 | bytes 3149344 | tf_op jit(solution)/shard_map/ij,pmjk->pmik/dot_general | solution.py:51
  27.3 1.1 copy.49
  28.4 0.0 all-to-all-done
  28.4 3.6 %all-to-all-start.3 = ((bf16[8,4,2,64,128]{4,3,1,0,2:T(8,128)(2,1)}), bf16[8,4,2,64,128]{4,3,1,0,2:T(8,128)(2,1)S(1)}, u32[]{:S(2)}, u32[]{:S(2)}) async-start(bf16[8,4,2,64,128]{4,3,1,0,2:T(8,128)(2,1)} %copy.49), calls=%async_computation.3 | async-start | bytes 2097152 | tf_op jit(solution)/shard_map/all_to_all | solution.py:57
  32.0 0.1 copy.59
  32.1 0.6 gather_fusion
  32.6 0.1 copy.42
  32.7 0.7 copy.43
  33.4 0.3 all-to-all-done.3
  33.7 0.0 copy-start.1
  33.7 5.1 %all-to-all-start.1 = ((s32[16,1,1,4]{3,2,1,0:T(1,128)}), s32[16,1,1,4]{3,2,1,0:T(1,128)}, u32[]{:S(2)}, u32[]{:S(2)}) async-start(s32[16,1,1,4]{3,2,1,0:T(1,128)} %copy.43), calls=%async_computation.1 | async-start | bytes 16384 | tf_op jit(solution)/shard_map/all_to_all | solution.py:73
  38.9 0.0 copy-done.1
  38.9 2.0 %gather_fusion.3 = bf16[16,4,64,128]{3,2,1,0:T(8,128)(2,1)S(1)} fusion(bf16[16,4,64,128]{3,2,1,0:T(8,128)(2,1)} %bitcast.65, s32[1024]{0:T(1024)S(1)} %pad_clamp_fusion), kind=kCustom, calls=%fused_computation.3 | custom fusion | bytes 2097216 | tf_op jit(solution)/shard_map/jit(_take)/gather | solution.py:60
  40.8 1.1 fusion.5
  42.0 3.2 %all-to-all-done.1 = s32[16,1,1,4]{3,2,1,0:T(1,128)} async-done(((s32[16,1,1,4]{3,2,1,0:T(1,128)}), s32[16,1,1,4]{3,2,1,0:T(1,128)}, u32[]{:S(2)}, u32[]{:S(2)}) %all-to-all-start.1) | async-done | bytes 288 | tf_op jit(solution)/shard_map/all_to_all | solution.py:73
  45.2 18.6 %all_to_all.78 = bf16[16,1,1,4,64,128]{5,4,3,2,1,0:T(8,128)(2,1)S(1)} all-to-all(bf16[16,1,1,4,64,128]{5,4,3,2,1,0:T(8,128)(2,1)} %fusion.5), channel_id=1, replica_groups=mesh['expert'=16,'tensor'=8,'replica'=2] {'expert'}, dimensions={0} | all-to-all | bytes 2097152 | tf_op jit(solution)/shard_map/all_to_all | solution.py:66
  63.8 32.6 %all_to_all.79 = bf16[1,1,16,4,64,128]{5,4,3,1,0,2:T(8,128)(2,1)} all-to-all(bf16[1,1,16,4,64,128]{5,4,3,1,0,2:T(8,128)(2,1)S(1)} %bitcast.66), channel_id=1, replica_groups=mesh['expert'=16,'tensor'=8,'replica'=2] {'tensor'}, dimensions={2} | all-to-all | bytes 2097152 | tf_op jit(solution)/shard_map/all_to_all | solution.py:65
  96.3 4.3 %all-to-all-start.2 = ((s32[1,1,16,4]{3,1,0,2:T(1,128)}), s32[1,1,16,4]{3,1,0,2:T(1,128)S(1)}, u32[]{:S(2)}, u32[]{:S(2)}) async-start(s32[1,1,16,4]{3,1,0,2:T(1,128)} %bitcast.31), calls=%async_computation.2 | async-start | bytes 16384 | tf_op jit(solution)/shard_map/all_to_all | solution.py:72
  100.6 0.0 all-gather.2.cloned.1.call-start
  100.7 2.1 %copy.52 = bf16[1,1,16,4,64,128]{5,3,4,2,1,0:T(4,128)(2,1)S(1)} copy(bf16[1,1,16,4,64,128]{5,4,3,1,0,2:T(8,128)(2,1)} %all_to_all.79) | data formatting | bytes 2097152 | tf_op jit(solution)/shard_map/all_to_all | solution.py:65
  102.8 4.4 %all-to-all-done.2 = s32[1,1,16,4]{3,1,0,2:T(1,128)S(1)} async-done(((s32[1,1,16,4]{3,1,0,2:T(1,128)}), s32[1,1,16,4]{3,1,0,2:T(1,128)S(1)}, u32[]{:S(2)}, u32[]{:S(2)}) %all-to-all-start.2) | async-done | bytes 288 | tf_op jit(solution)/shard_map/all_to_all | solution.py:72
  107.2 1.3 convert_bitcast_fusion
  108.5 3.3 %copy.53 = bf16[1,8,7,64,2,1,128]{6,4,3,2,1,5,0:T(2,128)(2,1)} copy(bf16[1,8,7,64,2,1,128]{6,2,3,4,1,5,0:T(8,128)(2,1)S(1)} %convert_bitcast_fusion) | data formatting | bytes 3670016 | tf_op jit(solution)/shard_map/transpose | solution.py:88
  111.8 5.3 %reshape.227 = bf16[1,8,7,1,64,256]{5,4,2,1,3,0:T(8,128)(2,1)} reshape(bf16[1,8,7,64,2,1,128]{6,4,3,2,1,5,0:T(2,128)(2,1)} %copy.53) | data formatting | bytes 3670016 | tf_op jit(solution)/shard_map/reshape | solution.py:90
  117.1 0.0 all-gather.2.cloned.1.call-update
  117.1 16.8 %all-gather.2.cloned.1.call-done = bf16[1,8,7,2,64,256]{5,4,2,1,0,3:T(8,128)(2,1)} async-done(((bf16[1,8,7,1,64,256]{5,4,2,1,0,3:T(8,128)(2,1)}), bf16[1,8,7,2,64,256]{5,4,2,1,0,3:T(8,128)(2,1)}) %all-gather.2.cloned.1.call-update) | async-done | bytes 3670032 | tf_op jit(solution)/shard_map/all_gather | solution.py:91
  133.9 4.4 %copy.55 = bf16[1,8,7,2,64,256]{5,4,3,2,1,0:T(8,128)(2,1)} copy(bf16[1,8,7,2,64,256]{5,4,2,1,0,3:T(8,128)(2,1)} %all-gather.2.cloned.1.call-done) | data formatting | bytes 7340032 | tf_op jit(solution)/shard_map/all_gather | solution.py:91
  (11 shorter events, 0.1 us)
Async XLA Ops:
  6.5 11.8 %copy-start = (bf16[8,896,128]{2,1,0:T(8,128)(2,1)S(1)}, bf16[8,896,128]{2,1,0:T(8,128)(2,1)}, u32[]{:S(2)}) copy-start(bf16[8,896,128]{2,1,0:T(8,128)(2,1)} %param.5) | copy-start | bytes 5505028
  8.7 19.7 %all-to-all-start = ((s32[8,4,2]{0,1,2:T(4,128)}), s32[8,4,2]{0,1,2:T(4,128)S(1)}, u32[]{:S(2)}, u32[]{:S(2)}) async-start(s32[8,4,2]{0,1,2:T(4,128)} %broadcast_in_dim.55), calls=%async_computation | async-start | bytes 8192 | tf_op jit(solution)/shard_map/all_to_all | solution.py:58
  28.4 5.3 %all-to-all-start.3 = ((bf16[8,4,2,64,128]{4,3,1,0,2:T(8,128)(2,1)}), bf16[8,4,2,64,128]{4,3,1,0,2:T(8,128)(2,1)S(1)}, u32[]{:S(2)}, u32[]{:S(2)}) async-start(bf16[8,4,2,64,128]{4,3,1,0,2:T(8,128)(2,1)} %copy.49), calls=%async_computation.3 | async-start | bytes 2097152 | tf_op jit(solution)/shard_map/all_to_all | solution.py:57
  33.7 5.1 %copy-start.1 = (bf16[8,4,2,64,128]{4,3,1,0,2:T(8,128)(2,1)}, bf16[8,4,2,64,128]{4,3,1,0,2:T(8,128)(2,1)S(1)}, u32[]{:S(2)}) copy-start(bf16[8,4,2,64,128]{4,3,1,0,2:T(8,128)(2,1)S(1)} %all-to-all-done.3) | copy-start | bytes 3145732
  33.7 11.4 %all-to-all-start.1 = ((s32[16,1,1,4]{3,2,1,0:T(1,128)}), s32[16,1,1,4]{3,2,1,0:T(1,128)}, u32[]{:S(2)}, u32[]{:S(2)}) async-start(s32[16,1,1,4]{3,2,1,0:T(1,128)} %copy.43), calls=%async_computation.1 | async-start | bytes 16384 | tf_op jit(solution)/shard_map/all_to_all | solution.py:73
  96.3 10.8 %all-to-all-start.2 = ((s32[1,1,16,4]{3,1,0,2:T(1,128)}), s32[1,1,16,4]{3,1,0,2:T(1,128)S(1)}, u32[]{:S(2)}, u32[]{:S(2)}) async-start(s32[1,1,16,4]{3,1,0,2:T(1,128)} %bitcast.31), calls=%async_computation.2 | async-start | bytes 16384 | tf_op jit(solution)/shard_map/all_to_all | solution.py:72
  100.6 33.3 %all-gather.2.cloned.1.call-start = ((), (), s32[]{:S(2)}) async-start(), calls=%async_computation.6 | async-start | bytes 5505024 | tf_op jit(solution)/shard_map/all_gather | solution.py:91
Sparse Core Ops, SparseCore 0:
  117.2 16.6 all-gather.1
where the time goes:
time: 146 us; the launch traced here: 145 us
  blocking collectives  51.2 us (35%)
  local copies, waits for them, and re-layouts  26.8 us (18%)
  waiting for transfers between devices  24.8 us (17%)
  starting transfers between devices  19.4 us (13%)
  between operations  13.5 us (9%)
  other arithmetic  5.93 us (4%)
  matrix products  3.58 us (2%)
    all_to_all x1, blocking collectives, body(): lax.all_to_all(lax.all_to_all(chosen, 'expert', split_axis=0, concat_axis...  32.6 us
    all_to_all x1, blocking collectives, body(): lax.all_to_all(chosen, 'expert', split_axis=0, concat_axis=2, tiled=True)  18.6 us
    all_gather x1, waiting for transfers between devices, body(): whole_rows = lax.all_gather(owned_rows, 'replica', axis=3, tiled=True)  16.8 us
    all_to_all x1, starting transfers between devices, body(): lax.all_to_all(spots_pair, 'replica', split_axis=2, concat_axis=0, tiled=...  6.41 us
    reshape x1, local copies, waits for them, and re-layouts, body(): placed.reshape(owner_slots, source_count, block_rows, 1, part_rows, owner...  5.3 us
    all_to_all x1, starting transfers between devices, body(): lax.all_to_all(chosen_spots, 'expert', split_axis=0, concat_axis=2, tiled...  5.1 us
    all_to_all x1, waiting for transfers between devices, body(): lax.all_to_all(lax.all_to_all(chosen_spots, 'expert', split_axis=0, conca...  4.42 us
    all_gather x1, local copies, waits for them, and re-layouts, body(): whole_rows = lax.all_gather(owned_rows, 'replica', axis=3, tiled=True)  4.37 us
  transfers between devices with their start and end apart: 5, of which 4 were waited for; matrix products, arithmetic and copies ran while one was open for 14% of the time, Pallas kernels for 0%

commit v1 on v0

--- a/solution.py
+++ b/solution.py
@@ -88,7 +88,7 @@
     placed = jnp.transpose(placed, (0, 1, 3, 5, 2, 4, 6))
     owner_cols = members * block_cols * BLK
     owned_rows = placed.reshape(owner_slots, source_count, block_rows, 1, part_rows, owner_cols)
-    whole_rows = lax.all_gather(owned_rows, "replica", axis=3, tiled=True)
+    whole_rows = jnp.concatenate(lax.all_gather(owned_rows, "replica"), axis=3)
     return whole_rows.reshape(owner_slots, tensor_count * block_rows * BLK, owner_cols)
 
 

time: 146 us -> 146 us (level)
    another operation x0 -> x1, local copies, waits for them, and re-layouts: none -> 5.3 us  [body(): whole_rows = jnp.concatenate(lax.all_gather(owned_rows, 'replica'), axis=3)]
    reshape x1 -> x0, local copies, waits for them, and re-layouts: 5.3 us -> none  [body(): placed.reshape(owner_slots, source_count, block_rows, 1, part_rows, owner...]
where the time goes in v1:
time: 146 us; the launch traced here: 145 us
  blocking collectives  51.2 us (35%)
  local copies, waits for them, and re-layouts  26.8 us (18%)
  waiting for transfers between devices  24.8 us (17%)
  starting transfers between devices  19.4 us (13%)
  between operations  13.5 us (9%)
  other arithmetic  5.93 us (4%)
  matrix products  3.58 us (2%)
    all_to_all x1, blocking collectives, body(): lax.all_to_all(lax.all_to_all(chosen, 'expert', split_axis=0, concat_axis...  32.6 us
    all_to_all x1, blocking collectives, body(): lax.all_to_all(chosen, 'expert', split_axis=0, concat_axis=2, tiled=True)  18.6 us
    all_gather x1, waiting for transfers between devices, body(): whole_rows = jnp.concatenate(lax.all_gather(owned_rows, 'replica'), axis=3)  16.8 us
    all_to_all x1, starting transfers between devices, body(): lax.all_to_all(spots_pair, 'replica', split_axis=2, concat_axis=0, tiled=...  6.41 us
    another operation x1, local copies, waits for them, and re-layouts, body(): whole_rows = jnp.concatenate(lax.all_gather(owned_rows, 'replica'), axis=3)  5.3 us
    all_to_all x1, starting transfers between devices, body(): lax.all_to_all(chosen_spots, 'expert', split_axis=0, concat_axis=2, tiled...  5.1 us
    all_to_all x1, waiting for transfers between devices, body(): lax.all_to_all(lax.all_to_all(chosen_spots, 'expert', split_axis=0, conca...  4.42 us
    all_gather x1, local copies, waits for them, and re-layouts, body(): whole_rows = jnp.concatenate(lax.all_gather(owned_rows, 'replica'), axis=3)  4.37 us
  transfers between devices with their start and end apart: 5, of which 4 were waited for; matrix products, arithmetic and copies ran while one was open for 14% of the time, Pallas kernels for 0%

profile of v1, /device:TPU:1, one launch (start us, length us, event | category | flops | bytes accessed | tf_op | source)
XLA Modules:
  0.0 145.1 jit_solution(11660733728816668597)
XLA Ops:
  6.5 0.0 copy-start
  6.5 0.9 iota_select_fusion
  7.4 0.7 sort.17
  8.1 0.6 broadcast_in_dim.55
  8.7 6.4 %all-to-all-start = ((s32[8,4,2]{0,1,2:T(4,128)}), s32[8,4,2]{0,1,2:T(4,128)S(1)}, u32[]{:S(2)}, u32[]{:S(2)}) async-start(s32[8,4,2]{0,1,2:T(4,128)} %broadcast_in_dim.55), calls=%async_computation | async-start | bytes 8192 | tf_op jit(solution)/shard_map/all_to_all | solution.py:58
  15.1 0.7 compare_and_fusion
  15.8 0.7 compare_select_fusion.1
  16.4 0.8 copy.38
  17.2 0.1 copy.46
  17.3 0.1 reshape.257
  17.4 0.7 gather_fusion.4
  18.1 0.1 reshape.260
  18.1 0.1 copy.47
  18.2 0.1 copy.48
  18.3 0.0 copy-done
  18.3 0.8 gather_fusion.2
  19.1 4.0 %gather_fusion.1 = f32[32,128,128]{2,1,0:T(8,128)} fusion(f32[8,7,128,1,128]{4,2,1,0,3:T(8,128)} %bitcast.69, s32[32]{0:T(128)S(1)} %reshape.257), kind=kCustom, calls=%fused_computation.1 | custom fusion | bytes 4194688 | tf_op jit(solution)/shard_map/gather | solution.py:42
  23.2 1.9 %convert_subtract_fusion = f32[32,128,128]{2,1,0:T(8,128)S(1)} fusion(f32[32,128,128]{2,1,0:T(8,128)} %gather_fusion.1, bf16[32,128,128]{2,1,0:T(8,128)(2,1)S(1)} %gather_fusion.2), kind=kLoop, calls=%fused_computation.5 | loop fusion | flops 1048576 | bytes 5242880 | tf_op jit(solution)/shard_map/sub | solution.py:49
  25.0 2.3 %fusion.2 = bf16[8,4,128,128]{2,3,1,0:T(8,128)(2,1)S(1)} fusion(f32[8,4,128,128]{3,2,1,0:T(8,128)S(1)} %bitcast.63, pred[8,4]{1,0:T(8,128)(4,1)S(1)} %copy.48, s32[128]{0:T(128)S(1)} %get-tuple-element.7, s32[128]{0:T(128)S(1)} %get-tuple-element.8, s32[128]{0:T(128)S(1)} %get-tuple-element.9, s32[128]{0:T(128)S(1)} %get-tuple-element.10, ...), kind=kOutput, calls=%fused_computation.9 | convolution fusion | flops 806813696 | bytes 3149344 | tf_op jit(solution)/shard_map/ij,pmjk->pmik/dot_general | solution.py:51
  27.3 1.1 copy.49
  28.4 0.0 all-to-all-done
  28.4 3.6 %all-to-all-start.3 = ((bf16[8,4,2,64,128]{4,3,1,0,2:T(8,128)(2,1)}), bf16[8,4,2,64,128]{4,3,1,0,2:T(8,128)(2,1)S(1)}, u32[]{:S(2)}, u32[]{:S(2)}) async-start(bf16[8,4,2,64,128]{4,3,1,0,2:T(8,128)(2,1)} %copy.49), calls=%async_computation.3 | async-start | bytes 2097152 | tf_op jit(solution)/shard_map/all_to_all | solution.py:57
  32.0 0.1 copy.59
  32.1 0.6 gather_fusion
  32.6 0.1 copy.42
  32.7 0.7 copy.43
  33.4 0.3 all-to-all-done.3
  33.7 0.0 copy-start.1
  33.7 5.1 %all-to-all-start.1 = ((s32[16,1,1,4]{3,2,1,0:T(1,128)}), s32[16,1,1,4]{3,2,1,0:T(1,128)}, u32[]{:S(2)}, u32[]{:S(2)}) async-start(s32[16,1,1,4]{3,2,1,0:T(1,128)} %copy.43), calls=%async_computation.1 | async-start | bytes 16384 | tf_op jit(solution)/shard_map/all_to_all | solution.py:73
  38.9 0.0 copy-done.1
  38.9 2.0 %gather_fusion.3 = bf16[16,4,64,128]{3,2,1,0:T(8,128)(2,1)S(1)} fusion(bf16[16,4,64,128]{3,2,1,0:T(8,128)(2,1)} %bitcast.67, s32[1024]{0:T(1024)S(1)} %pad_clamp_fusion), kind=kCustom, calls=%fused_computation.3 | custom fusion | bytes 2097216 | tf_op jit(solution)/shard_map/jit(_take)/gather | solution.py:60
  40.8 1.1 fusion.5
  42.0 3.2 %all-to-all-done.1 = s32[16,1,1,4]{3,2,1,0:T(1,128)} async-done(((s32[16,1,1,4]{3,2,1,0:T(1,128)}), s32[16,1,1,4]{3,2,1,0:T(1,128)}, u32[]{:S(2)}, u32[]{:S(2)}) %all-to-all-start.1) | async-done | bytes 288 | tf_op jit(solution)/shard_map/all_to_all | solution.py:73
  45.2 18.6 %all_to_all.78 = bf16[16,1,1,4,64,128]{5,4,3,2,1,0:T(8,128)(2,1)S(1)} all-to-all(bf16[16,1,1,4,64,128]{5,4,3,2,1,0:T(8,128)(2,1)} %fusion.5), channel_id=1, replica_groups=mesh['expert'=16,'tensor'=8,'replica'=2] {'expert'}, dimensions={0} | all-to-all | bytes 2097152 | tf_op jit(solution)/shard_map/all_to_all | solution.py:66
  63.8 32.6 %all_to_all.79 = bf16[1,1,16,4,64,128]{5,4,3,1,0,2:T(8,128)(2,1)} all-to-all(bf16[1,1,16,4,64,128]{5,4,3,1,0,2:T(8,128)(2,1)S(1)} %bitcast.68), channel_id=1, replica_groups=mesh['expert'=16,'tensor'=8,'replica'=2] {'tensor'}, dimensions={2} | all-to-all | bytes 2097152 | tf_op jit(solution)/shard_map/all_to_all | solution.py:65
  96.3 4.3 %all-to-all-start.2 = ((s32[1,1,16,4]{3,1,0,2:T(1,128)}), s32[1,1,16,4]{3,1,0,2:T(1,128)S(1)}, u32[]{:S(2)}, u32[]{:S(2)}) async-start(s32[1,1,16,4]{3,1,0,2:T(1,128)} %bitcast.32), calls=%async_computation.2 | async-start | bytes 16384 | tf_op jit(solution)/shard_map/all_to_all | solution.py:72
  100.6 0.0 all-gather.2.cloned.1.call-start
  100.7 2.1 %copy.52 = bf16[1,1,16,4,64,128]{5,3,4,2,1,0:T(4,128)(2,1)S(1)} copy(bf16[1,1,16,4,64,128]{5,4,3,1,0,2:T(8,128)(2,1)} %all_to_all.79) | data formatting | bytes 2097152 | tf_op jit(solution)/shard_map/all_to_all | solution.py:65
  102.8 4.4 %all-to-all-done.2 = s32[1,1,16,4]{3,1,0,2:T(1,128)S(1)} async-done(((s32[1,1,16,4]{3,1,0,2:T(1,128)}), s32[1,1,16,4]{3,1,0,2:T(1,128)S(1)}, u32[]{:S(2)}, u32[]{:S(2)}) %all-to-all-start.2) | async-done | bytes 288 | tf_op jit(solution)/shard_map/all_to_all | solution.py:72
  107.2 1.3 convert_bitcast_fusion
  108.5 3.3 %copy.53 = bf16[1,8,7,64,2,1,128]{6,4,3,2,1,5,0:T(2,128)(2,1)} copy(bf16[1,8,7,64,2,1,128]{6,2,3,4,1,5,0:T(8,128)(2,1)S(1)} %convert_bitcast_fusion) | data formatting | bytes 3670016 | tf_op jit(solution)/shard_map/transpose | solution.py:88
  111.8 5.3 %all_gather_reshape.3 = bf16[1,1,8,7,1,64,256]{6,5,3,2,4,1,0:T(8,128)(2,1)} reshape(bf16[1,8,7,64,2,1,128]{6,4,3,2,1,5,0:T(2,128)(2,1)} %copy.53) | data formatting | bytes 3670016 | tf_op jit(solution)/shard_map/all_gather;reshape | solution.py:91
  117.1 0.0 all-gather.2.cloned.1.call-update
  117.1 16.8 %all-gather.2.cloned.1.call-done = bf16[2,1,8,7,1,64,256]{6,5,4,3,2,1,0:T(8,128)(2,1)} async-done(((bf16[1,1,8,7,1,64,256]{6,5,4,3,2,1,0:T(8,128)(2,1)}), bf16[2,1,8,7,1,64,256]{6,5,4,3,2,1,0:T(8,128)(2,1)}) %all-gather.2.cloned.1.call-update) | async-done | bytes 3670032 | tf_op jit(solution)/shard_map/all_gather | solution.py:91
  133.9 4.4 %copy.55 = bf16[2,1,8,7,1,64,256]{6,5,0,3,2,4,1:T(8,128)(2,1)} copy(bf16[2,1,8,7,1,64,256]{6,5,4,3,2,1,0:T(8,128)(2,1)} %all-gather.2.cloned.1.call-done) | data formatting | bytes 7340032 | tf_op jit(solution)/shard_map/all_gather | solution.py:91
  (11 shorter events, 0.1 us)
Async XLA Ops:
  6.5 11.8 %copy-start = (bf16[8,896,128]{2,1,0:T(8,128)(2,1)S(1)}, bf16[8,896,128]{2,1,0:T(8,128)(2,1)}, u32[]{:S(2)}) copy-start(bf16[8,896,128]{2,1,0:T(8,128)(2,1)} %param.5) | copy-start | bytes 5505028
  8.7 19.7 %all-to-all-start = ((s32[8,4,2]{0,1,2:T(4,128)}), s32[8,4,2]{0,1,2:T(4,128)S(1)}, u32[]{:S(2)}, u32[]{:S(2)}) async-start(s32[8,4,2]{0,1,2:T(4,128)} %broadcast_in_dim.55), calls=%async_computation | async-start | bytes 8192 | tf_op jit(solution)/shard_map/all_to_all | solution.py:58
  28.4 5.3 %all-to-all-start.3 = ((bf16[8,4,2,64,128]{4,3,1,0,2:T(8,128)(2,1)}), bf16[8,4,2,64,128]{4,3,1,0,2:T(8,128)(2,1)S(1)}, u32[]{:S(2)}, u32[]{:S(2)}) async-start(bf16[8,4,2,64,128]{4,3,1,0,2:T(8,128)(2,1)} %copy.49), calls=%async_computation.3 | async-start | bytes 2097152 | tf_op jit(solution)/shard_map/all_to_all | solution.py:57
  33.7 5.1 %copy-start.1 = (bf16[8,4,2,64,128]{4,3,1,0,2:T(8,128)(2,1)}, bf16[8,4,2,64,128]{4,3,1,0,2:T(8,128)(2,1)S(1)}, u32[]{:S(2)}) copy-start(bf16[8,4,2,64,128]{4,3,1,0,2:T(8,128)(2,1)S(1)} %all-to-all-done.3) | copy-start | bytes 3145732
  33.7 11.4 %all-to-all-start.1 = ((s32[16,1,1,4]{3,2,1,0:T(1,128)}), s32[16,1,1,4]{3,2,1,0:T(1,128)}, u32[]{:S(2)}, u32[]{:S(2)}) async-start(s32[16,1,1,4]{3,2,1,0:T(1,128)} %copy.43), calls=%async_computation.1 | async-start | bytes 16384 | tf_op jit(solution)/shard_map/all_to_all | solution.py:73
  96.3 10.8 %all-to-all-start.2 = ((s32[1,1,16,4]{3,1,0,2:T(1,128)}), s32[1,1,16,4]{3,1,0,2:T(1,128)S(1)}, u32[]{:S(2)}, u32[]{:S(2)}) async-start(s32[1,1,16,4]{3,1,0,2:T(1,128)} %bitcast.32), calls=%async_computation.2 | async-start | bytes 16384 | tf_op jit(solution)/shard_map/all_to_all | solution.py:72
  100.6 33.3 %all-gather.2.cloned.1.call-start = ((), (), s32[]{:S(2)}) async-start(), calls=%async_computation.6 | async-start | bytes 5505024 | tf_op jit(solution)/shard_map/all_gather | solution.py:91
Sparse Core Ops, SparseCore 0:
  117.2 16.6 all-gather.1
